TPU v7x, 32 devices: a whole 2x2x4 slice. The times are simulated.
32 devices in a mesh: seq: 8 (over z, y), rep: 4 (over x, core).
Axes of the slice: x: 2, y: 2, z: 4, core: 2. Of those that a mesh axis runs over, the one named last changes fastest.
Arguments:
- inputs: bfloat16 [4, 1024, 1024], P('rep', 'seq'), may hold values from -6 to 6
- weight_t: bfloat16 [3072, 1024], P('seq', 'rep'), may hold values from -0.1875 to 0.1875
- states: float32 [4, 1024, 1024], P('rep', 'seq'), may hold values from -0.9 to 0.9
- doc_ids: int32 [4, 1024], P('rep', 'seq'), may hold values from 0 to 3, never falling along the last dimension, each value on 1 to 512 neighbouring positions
- recur: float32 [3, 1024], replicated, may hold values from -1 to 1
- bias: float32 [3, 1024], replicated, may hold values from -8 to 3, as said below
- out_grad: bfloat16 [4, 1024, 1024], P('rep', 'seq'), may hold values from -6 to 6
Outputs:
- input_grad: bfloat16 [4, 1024, 1024], P('rep', 'seq')
- weight_grad: float32 [3072, 1024], P('seq', 'rep')
- param_grad: float32 [6, 1024], replicated
Inputs may be any that keep to these rules, and one draw needn't show every extreme that they name: `doc_ids`: within each sequence the numbers never fall; every document has 1 to 512 tokens, and some document has exactly 512. `bias`: row 0 lies between -8 and -1, rows 1 and 2 between -3 and 3.
All inputs are finite; a program needn't handle non-finite values.
Results may differ from a plain program's by a relative error of at most 0.0095.
Values may be sent and summed in bfloat16 or wider, within the bound.
A program may use at most 128 MiB of HBM per device.

v0:
```python
import math
import jax
import jax.numpy as jnp
from jax import lax
from jax.sharding import PartitionSpec as P


def shifted(block, axis, distance):
    devices = range(lax.axis_size(axis))
    route = [(i - distance, i) for i in devices if i - distance in devices]
    return lax.ppermute(block, axis, route)


def compose(earlier, later):
    return (later[0] * earlier[0], later[1] + later[0] * earlier[1])


def local(inputs, weight_t, states, doc_ids, recur, bias, out_grad):
    feats = inputs[0]
    hidden_now = states[0]
    ids_float = doc_ids[0].astype(jnp.float32)
    count = feats.shape[0]
    width = hidden_now.shape[1]
    columns = lax.all_gather(weight_t, "rep", axis=1, tiled=True)
    contract_last = (((1,), (1,)), ((), ()))
    full_weight = lax.all_gather(columns, "seq", axis=0, tiled=True)
    preact = lax.dot_general(feats, full_weight, contract_last, preferred_element_type=jnp.float32)
    tail_state, tail_id = shifted((hidden_now[-1:], ids_float[-1:]), "seq", 1)
    first_same = jnp.where(
        (ids_float[0] == tail_id[0]) & (lax.axis_index("seq") > 0), 1.0, 0.0
    ).astype(jnp.float32)
    same = jnp.concatenate(
        [first_same[None], (ids_float[1:] == ids_float[:-1]).astype(jnp.float32)]
    )
    prior = jnp.concatenate([tail_state, hidden_now[:-1]], 0) * same[:, None]
    gate_z = jax.nn.sigmoid(preact[:, :width] + recur[0] * prior + bias[0])
    gate_r = jax.nn.sigmoid(preact[:, width : 2 * width] + recur[1] * prior + bias[1])
    gate_c = jnp.tanh(preact[:, 2 * width :] + recur[2] * gate_r * prior + bias[2])
    jacobian = same[:, None] * (
        1.0
        - gate_z
        + (gate_c - prior) * gate_z * (1.0 - gate_z) * recur[0]
        + gate_z
        * (1.0 - gate_c * gate_c)
        * recur[2]
        * (gate_r + prior * gate_r * (1.0 - gate_r) * recur[1])
    )
    upstream = out_grad[0].astype(jnp.float32)
    jac_rows, up_rows = (
        lax.all_to_all(jacobian.T, "seq", split_axis=0, concat_axis=1, tiled=True),
        lax.all_to_all(upstream.T, "seq", split_axis=0, concat_axis=1, tiled=True),
    )
    factor = jnp.concatenate([jac_rows[:, 1:], jnp.zeros((jac_rows.shape[0], 1), jnp.float32)], 1)
    _, adjoint_rows = lax.associative_scan(compose, (factor, up_rows), reverse=True, axis=1)
    adjoint = lax.all_to_all(adjoint_rows, "seq", split_axis=1, concat_axis=0, tiled=True).T
    grad_z = adjoint * (gate_c - prior) * gate_z * (1.0 - gate_z)
    grad_c = adjoint * gate_z * (1.0 - gate_c * gate_c)
    grad_r = grad_c * recur[2] * prior * gate_r * (1.0 - gate_r)
    grad_pre = jnp.concatenate([grad_z, grad_r, grad_c], 1).astype(jnp.bfloat16)
    input_grad = jnp.dot(grad_pre, full_weight, preferred_element_type=jnp.float32)
    tokens_all = count * inputs.shape[0] * lax.axis_size("seq") * lax.axis_size("rep")
    normal_factor = 1.0 / math.sqrt(tokens_all)
    row_share = lax.psum_scatter(
        lax.dot_general(
            grad_pre, feats, (((0,), (0,)), ((), ())), preferred_element_type=jnp.float32
        ),
        "seq",
        scatter_dimension=0,
        tiled=True,
    )
    weight_grad = (
        lax.psum_scatter(
            row_share.astype(jnp.bfloat16), "rep", scatter_dimension=1, tiled=True
        ).astype(jnp.float32)
        * normal_factor
    )
    stats = jnp.stack(
        [
            grad_z.sum(0),
            grad_r.sum(0),
            grad_c.sum(0),
            (grad_z * prior).sum(0),
            (grad_r * prior).sum(0),
            (grad_c * gate_r * prior).sum(0),
        ]
    )
    param_grad = lax.psum(stats, ("seq", "rep")) * normal_factor
    return (input_grad.astype(jnp.bfloat16)[None], weight_grad, param_grad)


def solution(mesh):
    placed = (
        P("rep", "seq", None),
        P("seq", "rep"),
        P("rep", "seq", None),
        P("rep", "seq"),
        P(),
        P(),
        P("rep", "seq", None),
    )
    return jax.shard_map(
        local,
        mesh=mesh,
        in_specs=placed,
        out_specs=(P("rep", "seq", None), P("seq", "rep"), P()),
        check_vma=False,
    )
```

profile of v0, /device:TPU:0, one launch (start us, length us, event | category | flops | bytes accessed | tf_op | source)
XLA Modules:
  0.0 491.4 jit_solution(18385137196122489823)
XLA Ops:
  7.3 11.8 %all_gather.6 = bf16[384,1024]{1,0:T(8,128)(2,1)} all-gather(bf16[384,256]{1,0:T(8,128)(2,1)} %param.8), channel_id=1, replica_groups=mesh['seq'=8,'rep'=4] {'rep'}, dimensions={1}, use_global_device_ids=true | all-gather | bytes 983040 | tf_op jit(solution)/shard_map/all_gather | solution.py:24
  19.7 4.0 collective-permute-start
  23.7 2.9 collective-permute-start.1
  27.6 4.8 all-to-all-start
  34.1 95.4 %all-gather.2.cloned.1.call-done = bf16[3072,1024]{1,0:T(8,128)(2,1)} async-done(((bf16[384,1024]{1,0:T(8,128)(2,1)}), bf16[3072,1024]{1,0:T(8,128)(2,1)}) %all-gather.2.cloned.1.call-update) | async-done | bytes 6291472 | tf_op jit(solution)/shard_map/all_gather | solution.py:26
  129.5 5.0 %fusion.21 = f32[128,3072]{1,0:T(8,128)S(1)} fusion(bf16[3072,1024]{1,0:T(8,128)(2,1)} %all-gather.2.cloned.1.call-done, bf16[1,128,1024]{2,1,0:T(8,128)(2,1)S(1)} %copy-done), kind=kOutput, calls=%fused_computation.40 | convolution fusion | flops 805306368 | bytes 8126464 | tf_op jit(solution)/shard_map/dot_general | solution.py:27
  134.5 1.6 copy_bitcast_fusion
  136.1 4.2 all-to-all-start.1
  140.5 1.4 slice.317
  143.2 1.9 slice.318
  145.1 1.3 slice.342
  146.5 1.3 slice.346
  147.8 5.9 %all-to-all-done.1 = f32[8,128,128]{1,2,0:T(8,128)} async-done(((f32[8,128,128]{1,2,0:T(8,128)}), f32[8,128,128]{1,2,0:T(8,128)}, u32[]{:S(2)}, u32[]{:S(2)}) %all-to-all-start.1) | async-done | bytes 524320 | tf_op jit(solution)/shard_map/all_to_all | solution.py:50
  153.7 1.1 slice.421
  154.8 1.4 slice.339
  156.2 1.4 slice.343
  158.0 2.9 slice.344
  160.9 1.3 slice.350
  162.2 1.2 fusion.34
  165.6 1.1 fusion.35
  176.2 1.2 pad.65
  184.8 1.9 slice.340
  199.4 1.0 pad.81
  201.4 3.4 rev.2
  204.9 17.3 %all_to_all.63 = f32[128,8,128]{0,2,1:T(8,128)S(1)} all-to-all(f32[128,8,128]{0,2,1:T(8,128)S(1)} %bitcast.86), channel_id=1, replica_groups=mesh['seq'=8,'rep'=4] {'seq'}, dimensions={1} | all-to-all | bytes 1048576 | tf_op jit(solution)/shard_map/all_to_all | solution.py:55
  222.2 1.0 multiply_reduce_fusion
  223.1 6.3 %fusion.18 = f32[3072,1024]{1,0:T(8,128)} fusion(bf16[128,1024]{1,0:T(8,128)(2,1)S(1)} %get-tuple-element.11, bf16[128,1024]{1,0:T(8,128)(2,1)S(1)} %get-tuple-element.10, bf16[128,1024]{1,0:T(8,128)(2,1)S(1)} %get-tuple-element.9, bf16[1,128,1024]{2,1,0:T(8,128)(2,1)S(1)} %copy-done), kind=kOutput, calls=%fused_computation.34 | convolution fusion | flops 807665664 | bytes 13631488 | tf_op jit(solution)/shard_map/dot_general | solution.py:64
  229.6 206.6 %reduce-scatter.3.cloned.1.call-done = f32[384,1024]{1,0:T(8,128)} async-done(((f32[3072,1024]{1,0:T(8,128)}), f32[384,1024]{1,0:T(8,128)}) %reduce-scatter.3.cloned.1.call-update) | async-done | bytes 1572880 | tf_op jit(solution)/shard_map/reduce_scatter | solution.py:63
  436.1 2.4 convert_element_type.29
  438.6 39.5 %psum.7 = f32[6,1024]{1,0:T(8,128)S(1)} all-reduce(f32[6,1024]{1,0:T(8,128)S(1)} %stack.27), channel_id=1, replica_groups=mesh['seq'=8,'rep'=4] {'seq','rep'}, use_global_device_ids=true, to_apply=%region_8.9 | all-reduce | flops 6144 | bytes 49152 | tf_op jit(solution)/shard_map/psum | solution.py:87
  478.7 4.5 fusion
  483.2 1.7 convert_multiply_fusion
  (183 shorter events, 37.2 us)
Async XLA Ops:
  7.2 122.3 %copy-start = (bf16[1,128,1024]{2,1,0:T(8,128)(2,1)S(1)}, bf16[1,128,1024]{2,1,0:T(8,128)(2,1)}, u32[]{:S(2)}) copy-start(bf16[1,128,1024]{2,1,0:T(8,128)(2,1)} %param.7) | copy-start | bytes 786436
  7.2 11.9 %copy-start.24 = (s32[1,128]{1,0:T(1,128)S(1)}, s32[1,128]{1,0:T(1,128)}, u32[]{:S(2)}) copy-start(s32[1,128]{1,0:T(1,128)} %param.10) | copy-start | bytes 1540
  7.2 16.5 %copy-start.1 = (f32[1,128,1024]{2,1,0:T(8,128)S(1)}, f32[1,128,1024]{2,1,0:T(8,128)}, u32[]{:S(2)}) copy-start(f32[1,128,1024]{2,1,0:T(8,128)} %param.9) | copy-start | bytes 1572868
  7.2 19.4 %copy-start.2 = (bf16[1,128,1024]{2,1,0:T(8,128)(2,1)S(1)}, bf16[1,128,1024]{2,1,0:T(8,128)(2,1)}, u32[]{:S(2)}) copy-start(bf16[1,128,1024]{2,1,0:T(8,128)(2,1)} %param.13) | copy-start | bytes 786436
  7.2 122.2 %all-gather.2.cloned.1.call-start = ((), (), s32[]{:S(2)}) async-start(), calls=%async_computation.5 | async-start | bytes 7077888 | tf_op jit(solution)/shard_map/all_gather | solution.py:26
  19.1 13.4 %copy-start.17 = (f32[3,1024]{1,0:T(4,128)S(1)}, f32[3,1024]{1,0:T(4,128)}, u32[]{:S(2)}) copy-start(f32[3,1024]{1,0:T(4,128)} %param.12) | copy-start | bytes 36868
  19.1 13.4 %copy-start.18 = (f32[3,1024]{1,0:T(4,128)S(1)}, f32[3,1024]{1,0:T(4,128)}, u32[]{:S(2)}) copy-start(f32[3,1024]{1,0:T(4,128)} %param.11) | copy-start | bytes 36868
  19.7 13.0 %collective-permute-start = (f32[1]{0:T(128)}, f32[1]{0:T(128)}, u32[]{:S(2)}, u32[]{:S(2)}) collective-permute-start(f32[1]{0:T(128)} %bitcast.6), channel_id=1, source_target_pairs={{0,4},{4,8},{8,12},{12,16},{16,20},{20,24},{24,28},{1,5},{5,9},{9,... | collective-permute-start | bytes 20 | tf_op jit(solution)/shard_map/ppermute | solution.py:11
  23.7 110.7 %collective-permute-start.1 = (f32[1,1024]{1,0:T(1,128)S(1)}, f32[1,1024]{1,0:T(1,128)S(1)}, u32[]{:S(2)}, u32[]{:S(2)}) collective-permute-start(f32[1,1024]{1,0:T(1,128)S(1)} %slice_bitcast_fusion.1), channel_id=1, source_target_pairs={{0,4},{4,8},{8,12},{12,16},{16,20},{20,24},{24,28},{1,5},{5,9},{9,... | collective-permute-start | bytes 12296 | tf_op jit(solution)/shard_map/ppermute | solution.py:11
  27.6 108.5 %all-to-all-start = ((f32[8,128,128]{2,1,0:T(8,128)}), f32[8,128,128]{2,1,0:T(8,128)S(1)}, u32[]{:S(2)}, u32[]{:S(2)}) async-start(f32[8,128,128]{2,1,0:T(8,128)} %bitcast.2), calls=%async_computation | async-start | bytes 1048576 | tf_op jit(solution)/shard_map/all_to_all | solution.py:51
  32.5 101.9 %copy-start.3 = (f32[1,1024]{1,0:T(1,128)}, f32[1,1024]{1,0:T(1,128)S(1)}, u32[]{:S(2)}) copy-start(f32[1,1024]{1,0:T(1,128)S(1)} %get-tuple-element.25) | copy-start | bytes 12292
  32.5 101.9 %copy-start.5 = (f32[1,1024]{1,0:T(1,128)}, f32[1,1024]{1,0:T(1,128)S(1)}, u32[]{:S(2)}) copy-start(f32[1,1024]{1,0:T(1,128)S(1)} %get-tuple-element.26) | copy-start | bytes 12292
  32.5 101.9 %copy-start.7 = (f32[1,1024]{1,0:T(1,128)}, f32[1,1024]{1,0:T(1,128)S(1)}, u32[]{:S(2)}) copy-start(f32[1,1024]{1,0:T(1,128)S(1)} %get-tuple-element.27) | copy-start | bytes 12292
  32.6 101.9 %copy-start.9 = (f32[1,1024]{1,0:T(1,128)}, f32[1,1024]{1,0:T(1,128)S(1)}, u32[]{:S(2)}) copy-start(f32[1,1024]{1,0:T(1,128)S(1)} %get-tuple-element.22) | copy-start | bytes 12292
  32.6 101.9 %copy-start.11 = (f32[1,1024]{1,0:T(1,128)}, f32[1,1024]{1,0:T(1,128)S(1)}, u32[]{:S(2)}) copy-start(f32[1,1024]{1,0:T(1,128)S(1)} %get-tuple-element.23) | copy-start | bytes 12292
  32.6 101.9 %copy-start.13 = (f32[1,1024]{1,0:T(1,128)}, f32[1,1024]{1,0:T(1,128)S(1)}, u32[]{:S(2)}) copy-start(f32[1,1024]{1,0:T(1,128)S(1)} %get-tuple-element.24) | copy-start | bytes 12292
  34.1 100.5 %copy-start.19 = (f32[128]{0:T(128)}, f32[128]{0:T(128)S(1)}, u32[]{:S(2)}) copy-start(f32[128]{0:T(128)S(1)} %pad_maximum_fusion.12) | copy-start | bytes 1540
  134.4 1.7 copy-start.15
  136.1 17.6 %all-to-all-start.1 = ((f32[8,128,128]{1,2,0:T(8,128)}), f32[8,128,128]{1,2,0:T(8,128)}, u32[]{:S(2)}, u32[]{:S(2)}) async-start(f32[8,128,128]{1,2,0:T(8,128)} %copy_bitcast_fusion), calls=%async_computation.1 | async-start | bytes 1048576 | tf_op jit(solution)/shard_map/all_to_all | solution.py:50
  140.3 295.8 %reduce-scatter.3.cloned.1.call-start = ((), (), s32[]{:S(2)}) async-start(), calls=%async_computation.6 | async-start | bytes 14155776 | tf_op jit(solution)/shard_map/reduce_scatter | solution.py:63
  184.2 11.7 %copy-start.23 = (f32[128,1]{0,1:T(1,128)S(1)}, f32[128,1]{0,1:T(1,128)}, u32[]{:S(2)}) copy-start(f32[128,1]{0,1:T(1,128)} %slice.423) | copy-start | bytes 1540
  192.9 5.6 %copy-start.22 = (f32[128,1]{0,1:T(1,128)S(1)}, f32[128,1]{0,1:T(1,128)}, u32[]{:S(2)}) copy-start(f32[128,1]{0,1:T(1,128)} %slice.422) | copy-start | bytes 1540
  197.5 1.8 copy-start.21
  200.5 21.6 %copy-start.4 = (f32[1,1024]{1,0:T(1,128)S(1)}, f32[1,1024]{1,0:T(1,128)}, u32[]{:S(2)}) copy-start(f32[1,1024]{1,0:T(1,128)} %copy-done.3) | copy-start | bytes 12292
  200.5 21.6 %copy-start.6 = (f32[1,1024]{1,0:T(1,128)S(1)}, f32[1,1024]{1,0:T(1,128)}, u32[]{:S(2)}) copy-start(f32[1,1024]{1,0:T(1,128)} %copy-done.5) | copy-start | bytes 12292
  200.5 21.6 %copy-start.8 = (f32[1,1024]{1,0:T(1,128)S(1)}, f32[1,1024]{1,0:T(1,128)}, u32[]{:S(2)}) copy-start(f32[1,1024]{1,0:T(1,128)} %copy-done.7) | copy-start | bytes 12292
  200.5 21.6 %copy-start.10 = (f32[1,1024]{1,0:T(1,128)S(1)}, f32[1,1024]{1,0:T(1,128)}, u32[]{:S(2)}) copy-start(f32[1,1024]{1,0:T(1,128)} %copy-done.9) | copy-start | bytes 12292
  200.5 21.6 %copy-start.12 = (f32[1,1024]{1,0:T(1,128)S(1)}, f32[1,1024]{1,0:T(1,128)}, u32[]{:S(2)}) copy-start(f32[1,1024]{1,0:T(1,128)} %copy-done.11) | copy-start | bytes 12292
  200.5 21.6 %copy-start.14 = (f32[1,1024]{1,0:T(1,128)S(1)}, f32[1,1024]{1,0:T(1,128)}, u32[]{:S(2)}) copy-start(f32[1,1024]{1,0:T(1,128)} %copy-done.13) | copy-start | bytes 12292
  200.5 21.6 %copy-start.16 = (f32[1,1024]{1,0:T(1,128)S(1)}, f32[1,1024]{1,0:T(1,128)}, u32[]{:S(2)}) copy-start(f32[1,1024]{1,0:T(1,128)} %copy-done.15) | copy-start | bytes 12292
  200.6 21.6 %copy-start.20 = (f32[128]{0:T(128)S(1)}, f32[128]{0:T(128)}, u32[]{:S(2)}) copy-start(f32[128]{0:T(128)} %copy-done.19) | copy-start | bytes 1540
  229.5 253.7 %reduce-scatter.5.cloned.1.call-start = ((), (), s32[]{:S(2)}) async-start(), calls=%async_computation.7 | async-start | bytes 983040 | tf_op jit(solution)/shard_map/reduce_scatter | solution.py:72
Sparse Core Ops, SparseCore 0:
  19.2 110.1 all-gather.1
  229.6 206.4 reduce-scatter.2
  438.7 22.3 reduce-scatter.4
where the time goes:
time: 493 us; the launch traced here: 491 us
  waiting for transfers between devices  308 us (62%)
  blocking collectives  68.6 us (14%)
  local copies, waits for them, and re-layouts  42.2 us (9%)
  other arithmetic  25.3 us (5%)
  starting transfers between devices  16 us (3%)
  matrix products  15.8 us (3%)
  between operations  15.7 us (3%)
    reduce_scatter x1, waiting for transfers between devices, local(): lax.psum_scatter(lax.dot_general(grad_pre, feats, (((0,), (0,)), ((), ())...  207 us
    all_gather x1, waiting for transfers between devices, local(): full_weight = lax.all_gather(columns, 'seq', axis=0, tiled=True)  95.4 us
    psum x1, blocking collectives, local(): param_grad = lax.psum(stats, ('seq', 'rep')) * normal_factor  39.5 us
    slice x66, local copies, waits for them, and re-layouts, local(): lax.associative_scan(compose, (factor, up_rows), reverse=True, axis=1)  33.1 us
    all_to_all x1, blocking collectives, local(): lax.all_to_all(adjoint_rows, 'seq', split_axis=1, concat_axis=0, tiled=True)  17.3 us
    all_gather x1, blocking collectives, local(): columns = lax.all_gather(weight_t, 'rep', axis=1, tiled=True)  11.8 us
  transfers between devices with their start and end apart: 7, of which 3 were waited for; matrix products, arithmetic and copies ran while one was open for 4% of the time, Pallas kernels for 0%

commit v1 on v0

--- a/solution.py
+++ b/solution.py
@@ -84,7 +84,7 @@
             (grad_c * gate_r * prior).sum(0),
         ]
     )
-    param_grad = lax.psum(stats, ("seq", "rep")) * normal_factor
+    param_grad = jnp.sum(lax.all_gather(stats, ("seq", "rep")), axis=0) * normal_factor
     return (input_grad.astype(jnp.bfloat16)[None], weight_grad, param_grad)
 
 

time: 493 us -> 548 us (1.11)
  local copies, waits for them, and re-layouts: 42.2 us -> 87 us
  other arithmetic: 25.3 us -> 32.8 us
    slice x66, local copies, waits for them, and re-layouts: 33.1 us -> 76.7 us  [local(): lax.associative_scan(compose, (factor, up_rows), reverse=True, axis=1)]
    all_gather x0 -> x1, blocking collectives: none -> 42.6 us  [local(): lax.all_gather(stats, ('seq', 'rep'))]
    psum x1 -> x0, blocking collectives: 39.5 us -> none  [local(): param_grad = lax.psum(stats, ('seq', 'rep')) * normal_factor]
    mul x9, other arithmetic: 4.01 us -> 12 us  [compose(): return (later[0] * earlier[0], later[1] + later[0] * earlier[1])]
where the time goes in v1:
time: 548 us; the launch traced here: 544 us
  waiting for transfers between devices  305 us (56%)
  local copies, waits for them, and re-layouts  87 us (16%)
  blocking collectives  71.7 us (13%)
  other arithmetic  32.8 us (6%)
  starting transfers between devices  16 us (3%)
  matrix products  15.8 us (3%)
  between operations  15.7 us (3%)
    reduce_scatter x1, waiting for transfers between devices, local(): lax.psum_scatter(lax.dot_general(grad_pre, feats, (((0,), (0,)), ((), ())...  207 us
    all_gather x1, waiting for transfers between devices, local(): full_weight = lax.all_gather(columns, 'seq', axis=0, tiled=True)  95.4 us
    slice x66, local copies, waits for them, and re-layouts, local(): lax.associative_scan(compose, (factor, up_rows), reverse=True, axis=1)  76.7 us
    all_gather x1, blocking collectives, local(): lax.all_gather(stats, ('seq', 'rep'))  42.6 us
    all_to_all x1, blocking collectives, local(): lax.all_to_all(adjoint_rows, 'seq', split_axis=1, concat_axis=0, tiled=True)  17.3 us
    mul x9, other arithmetic, compose(): return (later[0] * earlier[0], later[1] + later[0] * earlier[1])  12 us
    all_gather x1, blocking collectives, local(): columns = lax.all_gather(weight_t, 'rep', axis=1, tiled=True)  11.8 us
  transfers between devices with their start and end apart: 7, of which 3 were waited for; matrix products, arithmetic and copies ran while one was open for 4% of the time, Pallas kernels for 0%

profile of v1, /device:TPU:0, one launch (start us, length us, event | category | flops | bytes accessed | tf_op | source)
XLA Modules:
  0.0 544.3 jit_solution(4175189980046602193)
XLA Ops:
  7.3 11.8 %all_gather.12 = bf16[384,1024]{1,0:T(8,128)(2,1)} all-gather(bf16[384,256]{1,0:T(8,128)(2,1)} %param.8), channel_id=1, replica_groups=mesh['seq'=8,'rep'=4] {'rep'}, dimensions={1}, use_global_device_ids=true | all-gather | bytes 983040 | tf_op jit(solution)/shard_map/all_gather | solution.py:24
  19.7 4.0 collective-permute-start
  23.7 2.9 collective-permute-start.1
  27.6 4.8 all-to-all-start
  34.1 95.4 %all-gather.4.cloned.1.call-done = bf16[3072,1024]{1,0:T(8,128)(2,1)} async-done(((bf16[384,1024]{1,0:T(8,128)(2,1)}), bf16[3072,1024]{1,0:T(8,128)(2,1)}) %all-gather.4.cloned.1.call-update) | async-done | bytes 6291472 | tf_op jit(solution)/shard_map/all_gather | solution.py:26
  129.5 5.0 fusion.21
  134.5 1.6 copy_bitcast_fusion
  136.1 4.2 all-to-all-start.1
  144.2 1.9 slice.318
  146.1 2.9 slice.342
  150.3 3.4 all-to-all-done.1
  158.0 3.0 slice.344
  160.9 3.0 slice.350
  167.9 1.8 fusion.35
  169.7 1.5 slice.358
  171.2 1.5 slice.360
  172.8 1.5 slice.364
  176.2 1.6 fusion.36
  177.8 1.5 slice.367
  179.3 1.5 slice.371
  180.7 1.5 slice.366
  182.2 1.5 slice.368
  225.1 1.9 pad.65
  232.5 1.5 slice.363
  251.1 3.4 rev.2
  254.5 17.3 %all_to_all.63 = f32[128,8,128]{0,2,1:T(8,128)S(1)} all-to-all(f32[128,8,128]{0,2,1:T(8,128)S(1)} %bitcast.87), channel_id=1, replica_groups=mesh['seq'=8,'rep'=4] {'seq'}, dimensions={1} | all-to-all | bytes 1048576 | tf_op jit(solution)/shard_map/all_to_all | solution.py:55
  272.8 6.3 %fusion.18 = f32[3072,1024]{1,0:T(8,128)} fusion(bf16[128,1024]{1,0:T(8,128)(2,1)S(1)} %get-tuple-element.11, bf16[128,1024]{1,0:T(8,128)(2,1)S(1)} %get-tuple-element.10, bf16[128,1024]{1,0:T(8,128)(2,1)S(1)} %get-tuple-element.9, bf16[1,128,1024]{2,1,0:T(8,128)(2,1)S(1)} %copy-done), kind=kOutput, calls=%fused_computation.34 | convolution fusion | flops 807665664 | bytes 13631488 | tf_op jit(solution)/shard_map/dot_general | solution.py:64
  279.2 206.6 %reduce-scatter.3.cloned.1.call-done = f32[384,1024]{1,0:T(8,128)} async-done(((f32[3072,1024]{1,0:T(8,128)}), f32[384,1024]{1,0:T(8,128)}) %reduce-scatter.3.cloned.1.call-update) | async-done | bytes 1572880 | tf_op jit(solution)/shard_map/reduce_scatter | solution.py:63
  485.8 2.4 convert_element_type.29
  488.3 42.6 %all-gather.1 = f32[32,6,1024]{2,1,0:T(8,128)S(1)} all-gather(f32[1,6,1024]{2,1,0:T(8,128)S(1)} %bitcast.88), channel_id=2, replica_groups=mesh['seq'=8,'rep'=4] {'seq','rep'}, dimensions={0}, use_global_device_ids=true | all-gather | bytes 811008 | tf_op jit(solution)/shard_map/all_gather | solution.py:87
  531.6 4.5 fusion
  536.1 1.7 convert_multiply_fusion
  (184 shorter events, 83.0 us)
Async XLA Ops:
  7.2 122.3 %copy-start = (bf16[1,128,1024]{2,1,0:T(8,128)(2,1)S(1)}, bf16[1,128,1024]{2,1,0:T(8,128)(2,1)}, u32[]{:S(2)}) copy-start(bf16[1,128,1024]{2,1,0:T(8,128)(2,1)} %param.7) | copy-start | bytes 786436
  7.2 11.9 %copy-start.24 = (s32[1,128]{1,0:T(1,128)S(1)}, s32[1,128]{1,0:T(1,128)}, u32[]{:S(2)}) copy-start(s32[1,128]{1,0:T(1,128)} %param.10) | copy-start | bytes 1540
  7.2 16.5 %copy-start.1 = (f32[1,128,1024]{2,1,0:T(8,128)S(1)}, f32[1,128,1024]{2,1,0:T(8,128)}, u32[]{:S(2)}) copy-start(f32[1,128,1024]{2,1,0:T(8,128)} %param.9) | copy-start | bytes 1572868
  7.2 19.4 %copy-start.3 = (bf16[1,128,1024]{2,1,0:T(8,128)(2,1)S(1)}, bf16[1,128,1024]{2,1,0:T(8,128)(2,1)}, u32[]{:S(2)}) copy-start(bf16[1,128,1024]{2,1,0:T(8,128)(2,1)} %param.13) | copy-start | bytes 786436
  7.2 122.2 %all-gather.4.cloned.1.call-start = ((), (), s32[]{:S(2)}) async-start(), calls=%async_computation.5 | async-start | bytes 7077888 | tf_op jit(solution)/shard_map/all_gather | solution.py:26
  19.1 13.4 %copy-start.18 = (f32[3,1024]{1,0:T(4,128)S(1)}, f32[3,1024]{1,0:T(4,128)}, u32[]{:S(2)}) copy-start(f32[3,1024]{1,0:T(4,128)} %param.12) | copy-start | bytes 36868
  19.1 13.4 %copy-start.19 = (f32[3,1024]{1,0:T(4,128)S(1)}, f32[3,1024]{1,0:T(4,128)}, u32[]{:S(2)}) copy-start(f32[3,1024]{1,0:T(4,128)} %param.11) | copy-start | bytes 36868
  19.7 13.0 %collective-permute-start = (f32[1]{0:T(128)}, f32[1]{0:T(128)}, u32[]{:S(2)}, u32[]{:S(2)}) collective-permute-start(f32[1]{0:T(128)} %bitcast.6), channel_id=1, source_target_pairs={{0,4},{4,8},{8,12},{12,16},{16,20},{20,24},{24,28},{1,5},{5,9},{9,... | collective-permute-start | bytes 20 | tf_op jit(solution)/shard_map/ppermute | solution.py:11
  23.7 110.7 %collective-permute-start.1 = (f32[1,1024]{1,0:T(1,128)S(1)}, f32[1,1024]{1,0:T(1,128)S(1)}, u32[]{:S(2)}, u32[]{:S(2)}) collective-permute-start(f32[1,1024]{1,0:T(1,128)S(1)} %slice_bitcast_fusion.1), channel_id=1, source_target_pairs={{0,4},{4,8},{8,12},{12,16},{16,20},{20,24},{24,28},{1,5},{5,9},{9,... | collective-permute-start | bytes 12296 | tf_op jit(solution)/shard_map/ppermute | solution.py:11
  27.6 108.5 %all-to-all-start = ((f32[8,128,128]{2,1,0:T(8,128)}), f32[8,128,128]{2,1,0:T(8,128)S(1)}, u32[]{:S(2)}, u32[]{:S(2)}) async-start(f32[8,128,128]{2,1,0:T(8,128)} %bitcast.2), calls=%async_computation | async-start | bytes 1048576 | tf_op jit(solution)/shard_map/all_to_all | solution.py:51
  32.5 101.9 %copy-start.4 = (f32[1,1024]{1,0:T(1,128)}, f32[1,1024]{1,0:T(1,128)S(1)}, u32[]{:S(2)}) copy-start(f32[1,1024]{1,0:T(1,128)S(1)} %get-tuple-element.25) | copy-start | bytes 12292
  32.5 101.9 %copy-start.6 = (f32[1,1024]{1,0:T(1,128)}, f32[1,1024]{1,0:T(1,128)S(1)}, u32[]{:S(2)}) copy-start(f32[1,1024]{1,0:T(1,128)S(1)} %get-tuple-element.26) | copy-start | bytes 12292
  32.5 101.9 %copy-start.8 = (f32[1,1024]{1,0:T(1,128)}, f32[1,1024]{1,0:T(1,128)S(1)}, u32[]{:S(2)}) copy-start(f32[1,1024]{1,0:T(1,128)S(1)} %get-tuple-element.27) | copy-start | bytes 12292
  32.6 101.9 %copy-start.10 = (f32[1,1024]{1,0:T(1,128)}, f32[1,1024]{1,0:T(1,128)S(1)}, u32[]{:S(2)}) copy-start(f32[1,1024]{1,0:T(1,128)S(1)} %get-tuple-element.22) | copy-start | bytes 12292
  32.6 101.9 %copy-start.12 = (f32[1,1024]{1,0:T(1,128)}, f32[1,1024]{1,0:T(1,128)S(1)}, u32[]{:S(2)}) copy-start(f32[1,1024]{1,0:T(1,128)S(1)} %get-tuple-element.23) | copy-start | bytes 12292
  32.6 101.9 %copy-start.14 = (f32[1,1024]{1,0:T(1,128)}, f32[1,1024]{1,0:T(1,128)S(1)}, u32[]{:S(2)}) copy-start(f32[1,1024]{1,0:T(1,128)S(1)} %get-tuple-element.24) | copy-start | bytes 12292
  34.1 100.5 %copy-start.21 = (f32[128]{0:T(128)}, f32[128]{0:T(128)S(1)}, u32[]{:S(2)}) copy-start(f32[128]{0:T(128)S(1)} %pad_maximum_fusion.12) | copy-start | bytes 1540
  134.4 1.7 copy-start.16
  136.1 17.6 %all-to-all-start.1 = ((f32[8,128,128]{1,2,0:T(8,128)}), f32[8,128,128]{1,2,0:T(8,128)}, u32[]{:S(2)}, u32[]{:S(2)}) async-start(f32[8,128,128]{1,2,0:T(8,128)} %copy_bitcast_fusion), calls=%async_computation.1 | async-start | bytes 1048576 | tf_op jit(solution)/shard_map/all_to_all | solution.py:50
  140.3 345.5 %reduce-scatter.3.cloned.1.call-start = ((), (), s32[]{:S(2)}) async-start(), calls=%async_computation.6 | async-start | bytes 14155776 | tf_op jit(solution)/shard_map/reduce_scatter | solution.py:63
  223.2 0.6 copy-start.20
  237.2 7.4 %copy-start.2 = (f32[128,127]{0,1:T(8,128)S(1)}, f32[128,127]{0,1:T(8,128)}, u32[]{:S(2)}) copy-start(f32[128,127]{0,1:T(8,128)} %slice.358) | copy-start | bytes 195076
  247.2 1.8 copy-start.23
  250.2 21.6 %copy-start.5 = (f32[1,1024]{1,0:T(1,128)S(1)}, f32[1,1024]{1,0:T(1,128)}, u32[]{:S(2)}) copy-start(f32[1,1024]{1,0:T(1,128)} %copy-done.4) | copy-start | bytes 12292
  250.2 21.6 %copy-start.7 = (f32[1,1024]{1,0:T(1,128)S(1)}, f32[1,1024]{1,0:T(1,128)}, u32[]{:S(2)}) copy-start(f32[1,1024]{1,0:T(1,128)} %copy-done.6) | copy-start | bytes 12292
  250.2 21.6 %copy-start.9 = (f32[1,1024]{1,0:T(1,128)S(1)}, f32[1,1024]{1,0:T(1,128)}, u32[]{:S(2)}) copy-start(f32[1,1024]{1,0:T(1,128)} %copy-done.8) | copy-start | bytes 12292
  250.2 21.6 %copy-start.11 = (f32[1,1024]{1,0:T(1,128)S(1)}, f32[1,1024]{1,0:T(1,128)}, u32[]{:S(2)}) copy-start(f32[1,1024]{1,0:T(1,128)} %copy-done.10) | copy-start | bytes 12292
  250.2 21.6 %copy-start.13 = (f32[1,1024]{1,0:T(1,128)S(1)}, f32[1,1024]{1,0:T(1,128)}, u32[]{:S(2)}) copy-start(f32[1,1024]{1,0:T(1,128)} %copy-done.12) | copy-start | bytes 12292
  250.2 21.6 %copy-start.15 = (f32[1,1024]{1,0:T(1,128)S(1)}, f32[1,1024]{1,0:T(1,128)}, u32[]{:S(2)}) copy-start(f32[1,1024]{1,0:T(1,128)} %copy-done.14) | copy-start | bytes 12292
  250.2 21.6 %copy-start.17 = (f32[1,1024]{1,0:T(1,128)S(1)}, f32[1,1024]{1,0:T(1,128)}, u32[]{:S(2)}) copy-start(f32[1,1024]{1,0:T(1,128)} %copy-done.16) | copy-start | bytes 12292
  250.2 21.6 %copy-start.22 = (f32[128]{0:T(128)S(1)}, f32[128]{0:T(128)}, u32[]{:S(2)}) copy-start(f32[128]{0:T(128)} %copy-done.21) | copy-start | bytes 1540
  279.2 256.9 %reduce-scatter.5.cloned.1.call-start = ((), (), s32[]{:S(2)}) async-start(), calls=%async_computation.7 | async-start | bytes 983040 | tf_op jit(solution)/shard_map/reduce_scatter | solution.py:72
Sparse Core Ops, SparseCore 0:
  19.2 110.1 all-gather.3
  279.3 206.4 reduce-scatter.2
  488.4 23.7 reduce-scatter.4
